TPU v7x, 32 devices: a whole 2x2x4 slice. The times are simulated.
32 devices in a mesh: seq: 8 (over z, y), head: 4 (over x, core).
Axes of the slice: x: 2, y: 2, z: 4, core: 2. Of those that a mesh axis runs over, the one named last changes fastest.
Arguments:
- inputs: bfloat16 [2048, 5120], P('seq', 'head'), may hold values from -6 to 6
- time_step: float32 [80, 2048], P('head', 'seq'), may hold values from 0.01 to 0.3
- decay_rate: float32 [80], P('head'), may hold values from 0.0001 to 1
- input_map: bfloat16 [2048, 128], P('seq'), may hold values from -6 to 6
- output_map: bfloat16 [2048, 128], P('seq'), may hold values from -0.59765625 to 0.59765625
- output_grad: bfloat16 [2048, 5120], P('seq', 'head'), may hold values from -3 to 3
- span_states: float32 [8, 80, 64, 128], P('seq', 'head'), may hold values from -6 to 6
- resets: int32 [8], P('seq'), may hold values from 0 to 4095
Outputs:
- grad_inputs: bfloat16 [2048, 5120], P('seq', 'head')
- grad_input_map: float32 [2048, 128], P('seq')
- grad_rate: float32 [80], P('head')
Inputs may be any that keep to these rules, and one draw needn't show every extreme that they name: `resets`: A value p under 256 means that a document starts at position p of that span; a value of 256 or more means that none starts in it.
All inputs are finite; a program needn't handle non-finite values.
Results may differ from a plain program's by a relative error of at most 0.003.
Values sent between devices are 32-bit elements; how exact they have to be, the bound alone decides.
A program may use at most 64 MiB of HBM per device.

v0:
```python
import jax
import jax.numpy as jnp
from jax import lax
from jax.sharding import PartitionSpec as P

highest = lax.Precision.HIGHEST


def prepare(x_block, step_block, decay_rate, b_block, c_block, grad_block, start_state, reset_at):
    block_len = step_block.shape[1]
    positions = jnp.arange(block_len, dtype=jnp.int32)
    later_doc = positions >= reset_at
    no_reset = reset_at >= block_len
    elapsed = jnp.cumsum(step_block, axis=1)
    log_decay = -decay_rate[:, None] * elapsed
    joined = (later_doc[:, None] == later_doc[None, :]) & (positions[None, :] >= positions[:, None])
    log_gaps = log_decay[:, None, :] - log_decay[:, :, None]
    pair_weight = jnp.where(joined[None], jnp.exp(jnp.where(joined[None], log_gaps, 0.0)), 0.0)
    intersection = jnp.dot(b_block, c_block.T, preferred_element_type=jnp.float32)
    products = jnp.einsum("shp,uhp->hsu", x_block, grad_block, preferred_element_type=jnp.float32)
    mixing = (pair_weight * intersection[None]).astype(jnp.bfloat16)
    pair_terms = pair_weight * products
    paired = pair_terms.astype(jnp.bfloat16)
    dx_inner = jnp.einsum("hsu,uhp->shp", mixing, grad_block, preferred_element_type=jnp.float32)
    db_inner = jnp.einsum("hsu,un->hsn", paired, c_block, preferred_element_type=jnp.float32)
    start_weight = jnp.where(later_doc[None], 0.0, jnp.exp(log_decay))
    end_weight = jnp.where(
        (later_doc | no_reset)[None], jnp.exp(log_decay[:, -1:] - log_decay), 0.0
    )
    carry_gain = jnp.where(no_reset, jnp.exp(log_decay[:, -1]), 0.0)
    c_wide = c_block.astype(jnp.float32)
    grad_wide = grad_block.astype(jnp.float32)
    weighted_c = start_weight[:, :, None] * c_wide[None]
    boundary_grad = jnp.einsum("hun,uhp->hpn", weighted_c, grad_wide, precision=highest)
    state_read = jnp.einsum("uhp,hpn->hun", grad_wide, start_state, precision=highest)
    start_term = jnp.sum(state_read * c_wide[None], axis=2)
    inside_term = jnp.sum(
        pair_terms
        * intersection[None]
        * step_block[:, :, None]
        * (elapsed[:, None, :] - elapsed[:, :, None]),
        axis=(1, 2),
    )
    entry_term = jnp.sum(start_weight * elapsed * start_term, axis=1)
    return (
        carry_gain,
        boundary_grad,
        dx_inner,
        db_inner,
        inside_term + entry_term,
        end_weight,
        elapsed,
    )


def finish(prepared, x_block, step_block, b_block, start_state, carried):
    carry_gain, boundary_grad, dx_inner, db_inner, partial_rate, end_weight, elapsed = prepared
    b_wide = b_block.astype(jnp.float32)
    x_wide = x_block.astype(jnp.float32)
    carried_b = jnp.einsum("sn,hpn->shp", b_wide, carried, precision=highest)
    carried_x = jnp.einsum("shp,hpn->hsn", x_wide, carried, precision=highest)
    step_rows = step_block.T[:, :, None]
    end_rows = end_weight.T[:, :, None]
    grad_x = (step_rows * (dx_inner + end_rows * carried_b)).astype(jnp.bfloat16)
    grad_b = jnp.sum(
        step_block[:, :, None] * (db_inner + end_weight[:, :, None] * carried_x), axis=0
    )
    last_elapsed = elapsed[:, -1]
    leaving_term = jnp.sum(
        end_weight
        * step_block
        * (last_elapsed[:, None] - elapsed)
        * jnp.sum(carried_x * b_wide[None], axis=2),
        axis=1,
    )
    through_term = carry_gain * last_elapsed * jnp.sum(carried * start_state, axis=(1, 2))
    return (grad_x, grad_b, partial_rate + leaving_term + through_term)


def backward_step(running, members):
    grad_piece, gain_piece = members
    return (grad_piece + gain_piece[:, None] * running, running)


def body(inputs, time_step, decay_rate, input_map, output_map, output_grad, span_states, resets):
    length = time_step.shape[1]
    block_count = span_states.shape[0]
    block_len = length // block_count
    head_count = decay_rate.shape[0]
    head_width = inputs.shape[1] // head_count
    number = 0
    x_block = inputs.reshape(block_len, head_count, head_width)
    grad_block = output_grad.reshape(block_len, head_count, head_width)
    step_block = time_step
    b_block = input_map
    prepared = prepare(
        x_block,
        step_block,
        decay_rate,
        b_block,
        output_map,
        grad_block,
        span_states[number],
        resets[number],
    )
    pieces = [(prepared, x_block, step_block, b_block)]
    gain_total = jnp.ones((head_count,), jnp.float32)
    grad_total = jnp.zeros_like(span_states[0])
    for number in reversed(range(block_count)):
        gain_block, grad_block_sum = (pieces[number][0][0], pieces[number][0][1])
        grad_total = grad_block_sum + gain_block[:, None, None] * grad_total
        gain_total = gain_block * gain_total
    seq_count = lax.axis_size("seq")
    entries = grad_total.shape[1] * grad_total.shape[2]
    sliced = grad_total.reshape(head_count, seq_count, entries // seq_count)
    received = lax.all_to_all(sliced, "seq", split_axis=1, concat_axis=1, tiled=True)
    gains = lax.all_gather(gain_total[None], "seq", axis=0, tiled=True)
    ending, exclusive = lax.scan(
        backward_step,
        jnp.zeros_like(received[:, 0]),
        (jnp.transpose(received, (1, 0, 2)), gains),
        reverse=True,
    )
    returned = lax.all_to_all(
        jnp.transpose(exclusive, (1, 0, 2)), "seq", split_axis=1, concat_axis=1, tiled=True
    )
    incoming = returned.reshape(grad_total.shape)
    carried = incoming
    grad_x_list = [None] * block_count
    grad_b_list = [None] * block_count
    rate_total = jnp.zeros((head_count,), jnp.float32)
    for number in reversed(range(block_count)):
        prepared, x_block, step_block, b_block = pieces[number]
        grad_x, grad_b, rate_part = finish(
            prepared, x_block, step_block, b_block, span_states[number], carried
        )
        grad_x_list[number] = grad_x.reshape(block_len, head_count * head_width)
        grad_b_list[number] = grad_b
        rate_total = rate_part
        carried = prepared[1] + prepared[0][:, None, None] * carried
    grad_inputs = grad_x_list[0]
    grad_input_map = lax.psum(grad_b_list[0], "head")
    grad_rate = -lax.psum(rate_total, "seq")
    return (grad_inputs, grad_input_map, grad_rate)


def solution(mesh):
    in_specs = (
        P("seq", "head"),
        P("head", "seq"),
        P("head"),
        P("seq", None),
        P("seq", None),
        P("seq", "head"),
        P("seq", "head", None, None),
        P("seq"),
    )
    out_specs = (P("seq", "head"), P("seq", None), P("head"))
    return jax.shard_map(body, mesh=mesh, in_specs=in_specs, out_specs=out_specs, check_vma=False)
```

profile of v0, /device:TPU:0, one launch (start us, length us, event | category | flops | bytes accessed | tf_op | source)
XLA Modules:
  0.0 141.0 jit_solution(17333116644024165966)
XLA Ops:
  8.6 0.8 reshape.290
  11.2 0.9 copy.37
  12.2 1.4 copy.36
  13.6 1.7 %fusion.31 = f32[20,64,128]{2,1,0:T(8,128)S(1)} fusion(bf16[256,20,64]{0,2,1:T(8,128)(2,1)S(1)} %bitcast.80, f32[256,128]{0,1:T(8,128)S(1)} %copy.37, f32[20,256]{1,0:T(8,128)S(1)} %get-tuple-element.152, f32[20]{0:T(128)S(1)} %broadcast_multiply_fusion.1), kind=kOutput, calls=%fused_computation.38 | convolution fusion | flops 504135680 | bytes 1462352 | tf_op jit(solution)/shard_map/hun,uhp->hpn/dot_general | solution.py:34
  15.4 1.3 copy.39
  16.7 7.3 %all-to-all-start = ((f32[20,8,1024]{2,0,1:T(8,128)}), f32[20,8,1024]{2,0,1:T(8,128)S(1)}, u32[]{:S(2)}, u32[]{:S(2)}) async-start(f32[20,8,1024]{2,0,1:T(8,128)} %copy.39), calls=%async_computation | async-start | bytes 1572864 | tf_op jit(solution)/shard_map/all_to_all | solution.py:116
  25.6 26.1 %all-reduce = f32[160]{0:T(256)S(1)} all-reduce(f32[160]{0:T(256)S(1)} %dynamic-update-slice), channel_id=2, replica_groups=mesh['seq'=8,'head'=4] {'seq'}, use_global_device_ids=true, to_apply=%add | all-reduce | flops 160 | bytes 1280
  53.9 0.7 slice_reduce_fusion.1
  54.7 1.4 %fusion.37 = pred[256,256]{1,0:T(8,128)(4,1)} fusion(pred[256]{0:T(512)(128)(4,1)} %copy-done.10), kind=kLoop, calls=%fused_computation.42 | loop fusion | flops 196608 | bytes 65792 | tf_op jit(solution)/shard_map/and | solution.py:16
  56.1 1.8 %fusion.43 = f32[256,256]{1,0:T(8,128)} fusion(bf16[256,128]{1,0:T(8,128)(2,1)} %param.13, bf16[256,128]{1,0:T(8,128)(2,1)} %param.14), kind=kOutput, calls=%fused_computation.64 | convolution fusion | flops 16777216 | bytes 393216 | tf_op jit(solution)/shard_map/dot_general | solution.py:19
  57.9 1.0 broadcast_in_dim.97
  58.9 11.4 %while.17 = (s32[]{:T(128)}, f32[20,1024]{1,0:T(8,128)S(1)}, f32[8,20,1024]{2,1,0:T(8,128)}, f32[8,20,1024]{2,1,0:T(8,128)S(1)}, f32[8,20]{1,0:T(8,128)}, /*index=5*/s32[]{:T(128)}, s32[]{:T(128)}, s32[]{:T(128)}) while((s32[]{:T(128)}, f32[20,1024]{1,0:T(8,128)S(1)}, f32[8,20,1024]{2,1,0:T(8,128)}, f32[8,20,1024]{2,1,0:T(8,128)S(1)}, ...), condition=%wide.region_3.4_spmd.clone, body=%wide.region_2.3_spmd.clone.sunk | while | flops 81924 | bytes 426352 | solution.py:118
  60.3 0.7 fusion.55
  61.7 0.7 fusion.55
  63.1 0.7 fusion.55
  64.6 0.7 fusion.55
  66.0 0.7 fusion.55
  67.4 0.7 fusion.55
  68.9 0.7 fusion.55
  70.3 4.5 %all-to-all-start.1 = ((f32[20,8,1024]{2,0,1:T(8,128)}), f32[20,8,1024]{2,0,1:T(8,128)S(1)}, u32[]{:S(2)}, u32[]{:S(2)}) async-start(f32[20,8,1024]{2,0,1:T(8,128)} %bitcast.8), calls=%async_computation.1 | async-start | bytes 1572864 | tf_op jit(solution)/shard_map/all_to_all | solution.py:124
  74.8 2.8 %multiply_reduce_fusion.1 = f32[20,256]{1,0:T(8,128)} fusion(bf16[256,20,64]{0,2,1:T(8,128)(2,1)S(1)} %bitcast.81, f32[256,128]{0,1:T(8,128)} %copy-done.7, f32[1,20,64,128]{3,2,1,0:T(8,128)S(1)} %copy-done.2), kind=kOutput, calls=%fused_computation.17 | convolution fusion | flops 504622080 | bytes 1462272 | tf_op jit(solution)/shard_map/uhp,hpn->hun/dot_general | solution.py:35
  77.7 3.7 %fusion.21 = f32[256,20,64]{0,2,1:T(8,128)} fusion(bf16[256,20,64]{0,2,1:T(8,128)(2,1)S(1)} %bitcast.82, f32[256,256]{1,0:T(8,128)} %fusion.43, f32[20,256]{1,0:T(8,128)S(1)} %get-tuple-element.153, pred[256,256]{1,0:T(8,128)(4,1)} %fusion.37), kind=kOutput, calls=%fused_computation.29 | convolution fusion | flops 174325760 | bytes 2314240 | tf_op jit(solution)/shard_map/hsu,uhp->shp/dot_general | solution.py:24
  81.4 5.3 %multiply_reduce_fusion = (f32[20]{0:T(128)}, f32[20,256,256]{2,1,0:T(8,128)}) fusion(f32[20,256]{1,0:T(8,128)S(1)} %bitcast.86, f32[20,256]{1,0:T(8,128)S(1)} %copy-done.6, f32[256,256]{1,0:T(8,128)S(1)} %copy-done.5, f32[20,256]{1,0:T(8,128)S(1)} %get-tuple-element.153, pred[256,256]{1,0:T(8,128)(4,1)S(1)} %copy-done.8, ...), kind=kOutput, calls=%fused_computation.4 | convolution fusion | flops 179568624 | bytes 6942800 | tf_op jit(solution)/shard_map/shp,uhp->hsu/dot_general | solution.py:20
  86.8 5.5 %all-to-all-done.1 = f32[20,8,1024]{2,0,1:T(8,128)S(1)} async-done(((f32[20,8,1024]{2,0,1:T(8,128)}), f32[20,8,1024]{2,0,1:T(8,128)S(1)}, u32[]{:S(2)}, u32[]{:S(2)}) %all-to-all-start.1) | async-done | bytes 655392 | tf_op jit(solution)/shard_map/all_to_all | solution.py:124
  92.3 1.1 multiply_reduce_fusion.2
  93.4 2.8 %fusion.9 = (f32[20,256]{1,0:T(8,128)S(1)}, f32[20,128,256]{1,2,0:T(8,128)S(1)}) fusion(f32[256,128]{1,0:T(8,128)} %convert_element_type.21, f32[20,64,128]{2,1,0:T(8,128)S(1)} %reshape.294, bf16[256,20,64]{0,2,1:T(8,128)(2,1)S(1)} %bitcast.77), kind=kOutput, calls=%fused_computation.16 | convolution fusion | flops 504622080 | bytes 4083712 | tf_op jit(solution)/shard_map/shp,hpn->hsn/dot_general | solution.py:61
  96.5 5.2 %fusion.8 = f32[256,128]{1,0:T(8,128)} fusion(f32[20,128,256]{1,2,0:T(8,128)S(1)} %get-tuple-element.155, f32[20,256]{1,0:T(8,128)S(1)} %get-tuple-element.150, f32[20,256]{1,0:T(8,128)S(1)} %copy-done.6, f32[20,256,256]{2,1,0:T(8,128)} %get-tuple-element.157, f32[20,256]{1,0:T(8,128)S(1)} %get-tuple-element.153, pred[256,256]{1,0:T(8,128)(4,1)} %fusion.37, ...), kind=kOutput, calls=%fused_computation.15 | convolution fusion | flops 344686592 | bytes 8187904 | tf_op jit(solution)/shard_map/hsu,un->hsn/dot_general | solution.py:25
  101.8 0.7 fusion.25
  102.4 19.4 %psum.15 = f32[20]{0:T(128)S(1)} all-reduce(f32[20]{0:T(128)S(1)} %multiply_add_fusion), channel_id=1, replica_groups=mesh['seq'=8,'head'=4] {'seq'}, use_global_device_ids=true, to_apply=%region_12.13 | all-reduce | flops 20 | bytes 160 | tf_op jit(solution)/shard_map/psum | solution.py:143
  121.8 1.1 copy.44
  123.4 9.1 %all-reduce.3.cloned.1.call-done = f32[256,128]{1,0:T(8,128)} async-done(((f32[256,128]{1,0:T(8,128)}), f32[256,128]{1,0:T(8,128)}) %all-reduce.3.cloned.1.call-update) | async-done | bytes 131088 | tf_op jit(solution)/shard_map/psum | solution.py:142
  132.6 1.6 %copy.62 = f32[256,128]{1,0:T(8,128)} copy(f32[256,128]{1,0:T(8,128)} %all-reduce.3.cloned.1.call-done) | data formatting | bytes 262144
  (90 shorter events, 13.1 us)
Async XLA Ops:
  7.2 16.8 %copy-start.20 = (u32[32]{0:T(128)S(1)}, u32[32]{0:T(128)}, u32[]{:S(2)}) copy-start(u32[32]{0:T(128)} %constant.57) | copy-start | bytes 388
  7.2 45.2 %copy-start.3 = (bf16[256,128]{1,0:T(8,128)(2,1)S(1)}, bf16[256,128]{1,0:T(8,128)(2,1)}, u32[]{:S(2)}) copy-start(bf16[256,128]{1,0:T(8,128)(2,1)} %param.13) | copy-start | bytes 196612
  7.2 45.8 %copy-start.1 = (bf16[256,1280]{1,0:T(8,128)(2,1)S(1)}, bf16[256,1280]{1,0:T(8,128)(2,1)}, u32[]{:S(2)}) copy-start(bf16[256,1280]{1,0:T(8,128)(2,1)} %param.10) | copy-start | bytes 1966084
  7.2 46.0 %copy-start.2 = (f32[1,20,64,128]{3,2,1,0:T(8,128)S(1)}, f32[1,20,64,128]{3,2,1,0:T(8,128)}, u32[]{:S(2)}) copy-start(f32[1,20,64,128]{3,2,1,0:T(8,128)} %param.16) | copy-start | bytes 1966084
  8.6 43.7 %copy-start.14 = (f32[20]{0:T(128)}, f32[20]{0:T(128)S(1)}, u32[]{:S(2)}) copy-start(f32[20]{0:T(128)S(1)} %neg.7) | copy-start | bytes 244
  10.9 41.4 %copy-start.10 = (pred[256]{0:T(512)(128)(4,1)}, pred[256]{0:T(512)(128)(4,1)S(1)}, u32[]{:S(2)}) copy-start(pred[256]{0:T(512)(128)(4,1)S(1)} %get-tuple-element.158) | copy-start | bytes 772
  11.2 41.1 %copy-start.11 = (f32[20]{0:T(128)}, f32[20]{0:T(128)S(1)}, u32[]{:S(2)}) copy-start(f32[20]{0:T(128)S(1)} %get-tuple-element.137) | copy-start | bytes 244
  12.2 1.4 copy-start.7
  16.7 41.2 %all-to-all-start = ((f32[20,8,1024]{2,0,1:T(8,128)}), f32[20,8,1024]{2,0,1:T(8,128)S(1)}, u32[]{:S(2)}, u32[]{:S(2)}) async-start(f32[20,8,1024]{2,0,1:T(8,128)} %copy.39), calls=%async_computation | async-start | bytes 1572864 | tf_op jit(solution)/shard_map/all_to_all | solution.py:116
  70.3 22.0 %all-to-all-start.1 = ((f32[20,8,1024]{2,0,1:T(8,128)}), f32[20,8,1024]{2,0,1:T(8,128)S(1)}, u32[]{:S(2)}, u32[]{:S(2)}) async-start(f32[20,8,1024]{2,0,1:T(8,128)} %bitcast.8), calls=%async_computation.1 | async-start | bytes 1572864 | tf_op jit(solution)/shard_map/all_to_all | solution.py:124
  74.8 57.8 %all-reduce.3.cloned.1.call-start = ((), (), s32[]{:S(2)}) async-start(), calls=%async_computation.2 | async-start | bytes 262144 | tf_op jit(solution)/shard_map/psum | solution.py:142
  77.7 3.7 %copy-start.5 = (f32[256,256]{1,0:T(8,128)S(1)}, f32[256,256]{1,0:T(8,128)}, u32[]{:S(2)}) copy-start(f32[256,256]{1,0:T(8,128)} %fusion.43) | copy-start | bytes 786436
  77.7 3.7 %copy-start.6 = (f32[20,256]{1,0:T(8,128)S(1)}, f32[20,256]{1,0:T(8,128)}, u32[]{:S(2)}) copy-start(f32[20,256]{1,0:T(8,128)} %param.11) | copy-start | bytes 61444
  77.7 3.7 %copy-start.8 = (pred[256,256]{1,0:T(8,128)(4,1)S(1)}, pred[256,256]{1,0:T(8,128)(4,1)}, u32[]{:S(2)}) copy-start(pred[256,256]{1,0:T(8,128)(4,1)} %fusion.37) | copy-start | bytes 196612
  86.8 9.4 %copy-start.9 = (f32[20,256]{1,0:T(8,128)S(1)}, f32[20,256]{1,0:T(8,128)}, u32[]{:S(2)}) copy-start(f32[20,256]{1,0:T(8,128)} %multiply_reduce_fusion.1) | copy-start | bytes 61444
  86.8 9.4 %copy-start.12 = (f32[20]{0:T(128)S(1)}, f32[20]{0:T(128)}, u32[]{:S(2)}) copy-start(f32[20]{0:T(128)} %copy-done.11) | copy-start | bytes 244
  86.8 9.5 %copy-start.13 = (f32[20]{0:T(128)S(1)}, f32[20]{0:T(128)}, u32[]{:S(2)}) copy-start(f32[20]{0:T(128)} %slice_reduce_fusion.1) | copy-start | bytes 244
  86.8 9.5 %copy-start.15 = (f32[20]{0:T(128)S(1)}, f32[20]{0:T(128)}, u32[]{:S(2)}) copy-start(f32[20]{0:T(128)} %copy-done.14) | copy-start | bytes 244
  86.8 9.5 %copy-start.16 = (pred[256]{0:T(512)(128)(4,1)S(1)}, pred[256]{0:T(512)(128)(4,1)}, u32[]{:S(2)}) copy-start(pred[256]{0:T(512)(128)(4,1)} %get-tuple-element.159) | copy-start | bytes 772
  86.8 9.5 %copy-start.18 = (pred[256]{0:T(512)(128)(4,1)S(1)}, pred[256]{0:T(512)(128)(4,1)}, u32[]{:S(2)}) copy-start(pred[256]{0:T(512)(128)(4,1)} %compare_bitcast_fusion) | copy-start | bytes 772
  96.5 5.2 %copy-start.17 = (f32[20]{0:T(128)S(1)}, f32[20]{0:T(128)}, u32[]{:S(2)}) copy-start(f32[20]{0:T(128)} %get-tuple-element.148) | copy-start | bytes 244
  96.5 5.2 %copy-start.19 = (f32[20]{0:T(128)S(1)}, f32[20]{0:T(128)}, u32[]{:S(2)}) copy-start(f32[20]{0:T(128)} %get-tuple-element.156) | copy-start | bytes 244
  96.5 5.2 %copy-start = (f32[256,20,64]{0,2,1:T(8,128)S(1)}, f32[256,20,64]{0,2,1:T(8,128)}, u32[]{:S(2)}) copy-start(f32[256,20,64]{0,2,1:T(8,128)} %fusion.21) | copy-start | bytes 3932164
  96.5 5.2 %copy-start.4 = (bf16[256,128]{1,0:T(8,128)(2,1)S(1)}, bf16[256,128]{1,0:T(8,128)(2,1)}, u32[]{:S(2)}) copy-start(bf16[256,128]{1,0:T(8,128)(2,1)} %param.13) | copy-start | bytes 196612
Sparse Core Ops, SparseCore 0:
  101.8 30.7 all-reduce.2
where the time goes:
time: 142 us; the launch traced here: 141 us
  blocking collectives  45.5 us (32%)
  matrix products  24 us (17%)
  local copies, waits for them, and re-layouts  16.6 us (12%)
  between operations  15.8 us (11%)
  waiting for transfers between devices  14.6 us (10%)
  other arithmetic  12.4 us (9%)
  starting transfers between devices  11.9 us (8%)
    unnamed x1, blocking collectives  26.1 us
    psum x1, blocking collectives, body(): grad_rate = -lax.psum(rate_total, 'seq')  19.4 us
    psum x1, waiting for transfers between devices, body(): grad_input_map = lax.psum(grad_b_list[0], 'head')  9.15 us
    all_to_all x1, starting transfers between devices, body(): lax.all_to_all(sliced, 'seq', split_axis=1, concat_axis=1, tiled=True)  7.31 us
    mul x8, local copies, waits for them, and re-layouts, backward_step(): return (grad_piece + gain_piece[:, None] * running, running)  5.48 us
    all_to_all x1, waiting for transfers between devices, body(): lax.all_to_all(jnp.transpose(exclusive, (1, 0, 2)), 'seq', split_axis=1,...  5.48 us
    dot_general x1, matrix products, prepare(): jnp.einsum('shp,uhp->hsu', x_block, grad_block, preferred_element_type=jn...  5.34 us
    unnamed x51, local copies, waits for them, and re-layouts  5.26 us
  transfers between devices with their start and end apart: 3, of which 2 were waited for; matrix products, arithmetic and copies ran while one was open for 15% of the time, Pallas kernels for 0%

commit v1 on v0

--- a/solution.py
+++ b/solution.py
@@ -121,8 +121,14 @@
         (jnp.transpose(received, (1, 0, 2)), gains),
         reverse=True,
     )
-    returned = lax.all_to_all(
-        jnp.transpose(exclusive, (1, 0, 2)), "seq", split_axis=1, concat_axis=1, tiled=True
+    returned = jnp.concatenate(
+        lax.all_to_all(
+            jnp.stack(jnp.split(jnp.transpose(exclusive, (1, 0, 2)), lax.axis_size("seq"), axis=1)),
+            "seq",
+            0,
+            0,
+        ),
+        axis=1,
     )
     incoming = returned.reshape(grad_total.shape)
     carried = incoming

time: 142 us -> 135 us (0.951)
  other arithmetic: 12.4 us -> 5.51 us
  local copies, waits for them, and re-layouts: 16.6 us -> 22.8 us
  waiting for transfers between devices: 14.6 us -> 9.19 us
    dynamic_update_slice x0 -> x16, local copies, waits for them, and re-layouts: none -> 6.85 us  [body(): lax.scan(backward_step, jnp.zeros_like(received[:, 0]), (jnp.transpose(re...]
    unnamed x51 -> x40, local copies, waits for them, and re-layouts: 5.26 us -> 11 us
    mul x8, local copies, waits for them, and re-layouts: 5.48 us -> 0.08 us  [backward_step(): return (grad_piece + gain_piece[:, None] * running, running)]
    dynamic_update_slice x8 -> x0, other arithmetic: 5.13 us -> none  [body(): lax.scan(backward_step, jnp.zeros_like(received[:, 0]), (jnp.transpose(re...]
    all_to_all x1, waiting for transfers between devices: 5.48 us -> 1.82 us  [body(): lax.all_to_all(jnp.stack(jnp.split(jnp.transpose(exclusive, (1, 0, 2)), l...]
    psum x1, waiting for transfers between devices: 9.15 us -> 7.36 us  [body(): grad_input_map = lax.psum(grad_b_list[0], 'head')]
    dot_general x1, matrix products: 1.76 us -> 0.18 us  [prepare(): jnp.dot(b_block, c_block.T, preferred_element_type=jnp.float32)]
  transfers between devices with their start and end apart: 3 -> 3, of which waited for: 2 -> 2; matrix products, arithmetic and copies ran while one was open for 15% -> 14% of each run, Pallas kernels for 0% -> 0%
where the time goes in v1:
time: 135 us
  blocking collectives  45.9 us (34%)
  matrix products  23.3 us (17%)
  local copies, waits for them, and re-layouts  22.8 us (17%)
  between operations  15.7 us (12%)
  starting transfers between devices  12 us (9%)
  waiting for transfers between devices  9.19 us (7%)
  other arithmetic  5.51 us (4%)
    unnamed x1, blocking collectives  26.1 us
    psum x1, blocking collectives, body(): grad_rate = -lax.psum(rate_total, 'seq')  19.8 us
    unnamed x40, local copies, waits for them, and re-layouts  11 us
    psum x1, waiting for transfers between devices, body(): grad_input_map = lax.psum(grad_b_list[0], 'head')  7.36 us
    all_to_all x1, starting transfers between devices, body(): lax.all_to_all(sliced, 'seq', split_axis=1, concat_axis=1, tiled=True)  7.31 us
    dynamic_update_slice x16, local copies, waits for them, and re-layouts, body(): lax.scan(backward_step, jnp.zeros_like(received[:, 0]), (jnp.transpose(re...  6.85 us
    dot_general x1, matrix products, prepare(): jnp.einsum('shp,uhp->hsu', x_block, grad_block, preferred_element_type=jn...  5.34 us
    dot_general x1, matrix products, prepare(): jnp.einsum('hsu,un->hsn', paired, c_block, preferred_element_type=jnp.flo...  5.05 us
  transfers between devices with their start and end apart: 3, of which 2 were waited for; matrix products, arithmetic and copies ran while one was open for 14% of the time, Pallas kernels for 0%

profile of v1, /device:TPU:0, one launch (start us, length us, event | category | flops | bytes accessed | tf_op | source)
XLA Modules:
  0.0 134.8 jit_solution(1520236713082113705)
XLA Ops:
  8.6 0.8 reshape.290
  11.1 0.9 copy.54
  12.1 1.4 %copy.53 = bf16[256,1280]{0,1:T(8,128)(2,1)S(1)} copy(bf16[256,1280]{1,0:T(8,128)(2,1)} %param.15) | data formatting | bytes 1310720 | tf_op args[5]
  13.5 0.8 copy-done.2
  14.3 1.7 %fusion.30 = f32[20,64,128]{2,1,0:T(8,128)S(1)} fusion(bf16[256,20,64]{0,2,1:T(8,128)(2,1)S(1)} %bitcast.128, f32[256,128]{0,1:T(8,128)S(1)} %copy.54, f32[20,256]{1,0:T(8,128)S(1)} %get-tuple-element.155, f32[20]{0:T(128)S(1)} %broadcast_multiply_fusion.1), kind=kOutput, calls=%fused_computation.37 | convolution fusion | flops 504135680 | bytes 1462352 | tf_op jit(solution)/shard_map/hun,uhp->hpn/dot_general | solution.py:34
  16.2 1.3 copy.56
  17.4 7.3 %all-to-all-start = ((f32[20,8,1024]{2,0,1:T(8,128)}), f32[20,8,1024]{2,0,1:T(8,128)S(1)}, u32[]{:S(2)}, u32[]{:S(2)}) async-start(f32[20,8,1024]{2,0,1:T(8,128)} %copy.56), calls=%async_computation | async-start | bytes 1572864 | tf_op jit(solution)/shard_map/all_to_all | solution.py:116
  26.4 26.1 %all-reduce = f32[160]{0:T(256)S(1)} all-reduce(f32[160]{0:T(256)S(1)} %dynamic-update-slice), channel_id=2, replica_groups=mesh['seq'=8,'head'=4] {'seq'}, use_global_device_ids=true, to_apply=%add | all-reduce | flops 160 | bytes 1280
  54.1 7.9 %while.17 = (s32[]{:T(128)}, f32[20,1024]{1,0:T(8,128)S(1)}, f32[8,20,1024]{2,0,1:T(8,128)S(1)}, f32[8,20,1024]{2,1,0:T(8,128)S(1)}, f32[8,20]{1,0:T(8,128)S(1)}, /*index=5*/s32[]{:T(128)}, s32[]{:T(128)}, s32[]{:T(128)}) while((s32[]{:T(128)}, f32[20,1024]{1,0:T(8,128)S(1)}, f32[8,20,1024]{2,0,1:T(8,128)S(1)}, ...), condition=%wide.region_3.4_spmd.clone, body=%wide.region_2.3_spmd.clone.sunk | while | flops 61444 | bytes 655727 | solution.py:118
  54.3 0.8 dynamic_update_slice.12
  55.3 0.8 dynamic_update_slice.12
  56.3 0.8 dynamic_update_slice.12
  57.3 0.8 dynamic_update_slice.12
  58.3 0.8 dynamic_update_slice.12
  59.3 0.8 dynamic_update_slice.12
  60.3 0.8 dynamic_update_slice.12
  61.3 0.8 dynamic_update_slice.12
  63.4 0.7 fusion.42
  64.8 0.7 fusion.40
  67.6 4.5 %all-to-all-start.1 = ((f32[8,20,1,1024]{3,2,1,0:T(1,128)}), f32[8,20,1,1024]{3,2,1,0:T(1,128)S(1)}, u32[]{:S(2)}, u32[]{:S(2)}) async-start(f32[8,20,1,1024]{3,2,1,0:T(1,128)} %fusion.37), calls=%async_computation.1 | async-start | bytes 1310720 | tf_op jit(solution)/shard_map/all_to_all | solution.py:125
  72.4 3.2 %multiply_reduce_fusion.1 = f32[20,256]{1,0:T(8,128)} fusion(bf16[256,20,64]{0,2,1:T(8,128)(2,1)} %bitcast.129, f32[256,128]{0,1:T(8,128)} %copy-done.7, f32[1,20,64,128]{3,2,1,0:T(8,128)} %param.16), kind=kOutput, calls=%fused_computation.16 | convolution fusion | flops 504622080 | bytes 1462272 | tf_op jit(solution)/shard_map/uhp,hpn->hun/dot_general | solution.py:35
  75.6 3.9 %fusion.20 = f32[256,20,64]{0,2,1:T(8,128)} fusion(bf16[256,20,64]{0,2,1:T(8,128)(2,1)} %bitcast.130, f32[256,256]{1,0:T(8,128)S(1)} %fusion.50, f32[20,256]{1,0:T(8,128)S(1)} %get-tuple-element.156, pred[256,256]{1,0:T(8,128)(4,1)S(1)} %fusion.36), kind=kOutput, calls=%fused_computation.28 | convolution fusion | flops 174325760 | bytes 2314240 | tf_op jit(solution)/shard_map/hsu,uhp->shp/dot_general | solution.py:24
  79.5 5.3 %multiply_reduce_fusion = (f32[20]{0:T(128)}, f32[20,256,256]{2,1,0:T(8,128)}) fusion(f32[20,256]{1,0:T(8,128)S(1)} %bitcast.134, f32[20,256]{1,0:T(8,128)S(1)} %copy-done.6, f32[256,256]{1,0:T(8,128)S(1)} %fusion.50, f32[20,256]{1,0:T(8,128)S(1)} %get-tuple-element.156, pred[256,256]{1,0:T(8,128)(4,1)S(1)} %fusion.36, ...), kind=kOutput, calls=%fused_computation.3 | convolution fusion | flops 179568624 | bytes 6942800 | tf_op jit(solution)/shard_map/shp,uhp->hsu/dot_general | solution.py:20
  84.9 1.8 %all-to-all-done.1 = f32[8,20,1,1024]{3,2,1,0:T(1,128)S(1)} async-done(((f32[8,20,1,1024]{3,2,1,0:T(1,128)}), f32[8,20,1,1024]{3,2,1,0:T(1,128)S(1)}, u32[]{:S(2)}, u32[]{:S(2)}) %all-to-all-start.1) | async-done | bytes 655392 | tf_op jit(solution)/shard_map/all_to_all | solution.py:125
  87.2 1.9 %fusion.8 = (f32[20,256]{1,0:T(8,128)S(1)}, f32[20,128,256]{1,2,0:T(8,128)S(1)}) fusion(f32[256,128]{1,0:T(8,128)S(1)} %convert_element_type.21, f32[20,64,128]{2,1,0:T(8,128)S(1)} %reshape_reshape.3, bf16[256,20,64]{0,2,1:T(8,128)(2,1)S(1)} %bitcast.116), kind=kOutput, calls=%fused_computation.15 | convolution fusion | flops 504622080 | bytes 4083712 | tf_op jit(solution)/shard_map/shp,hpn->hsn/dot_general | solution.py:61
  89.0 0.9 multiply_reduce_fusion.4
  90.0 5.0 %fusion.7 = f32[256,128]{1,0:T(8,128)} fusion(f32[20,128,256]{1,2,0:T(8,128)S(1)} %get-tuple-element.158, f32[20,256]{1,0:T(8,128)S(1)} %get-tuple-element.153, f32[20,256]{1,0:T(8,128)S(1)} %copy-done.6, f32[20,256,256]{2,1,0:T(8,128)} %get-tuple-element.160, f32[20,256]{1,0:T(8,128)S(1)} %get-tuple-element.156, pred[256,256]{1,0:T(8,128)(4,1)} %copy-done.8, ...), kind=kOutput, calls=%fused_computation.14 | convolution fusion | flops 344686592 | bytes 8187904 | tf_op jit(solution)/shard_map/hsu,un->hsn/dot_general | solution.py:25
  95.6 2.0 %fusion.24 = bf16[256,20,64]{0,2,1:T(8,128)(2,1)S(1)} fusion(f32[256,20,64]{0,2,1:T(8,128)} %fusion.20, f32[20,64,128]{2,1,0:T(8,128)S(1)} %reshape_reshape.3, f32[256,20]{0,1:T(8,128)S(1)} %get-tuple-element.154, f32[256,20]{0,1:T(8,128)S(1)} %bitcast.136, bf16[256,128]{1,0:T(8,128)(2,1)S(1)} %copy-done.4), kind=kOutput, calls=%fused_computation.33 | convolution fusion | flops 504627200 | bytes 2727936 | tf_op jit(solution)/shard_map/sn,hpn->shp/dot_general | solution.py:60
  97.6 19.8 %psum.15 = f32[20]{0:T(128)S(1)} all-reduce(f32[20]{0:T(128)S(1)} %multiply_add_fusion), channel_id=1, replica_groups=mesh['seq'=8,'head'=4] {'seq'}, use_global_device_ids=true, to_apply=%region_12.13 | all-reduce | flops 20 | bytes 160 | tf_op jit(solution)/shard_map/psum | solution.py:149
  117.4 1.1 copy.61
  119.0 7.4 %all-reduce.3.cloned.1.call-done = f32[256,128]{1,0:T(8,128)} async-done(((f32[256,128]{1,0:T(8,128)}), f32[256,128]{1,0:T(8,128)}) %all-reduce.3.cloned.1.call-update) | async-done | bytes 131088 | tf_op jit(solution)/shard_map/psum | solution.py:148
  126.4 1.6 %copy.102 = f32[256,128]{1,0:T(8,128)} copy(f32[256,128]{1,0:T(8,128)} %all-reduce.3.cloned.1.call-done) | data formatting | bytes 262144
  (89 shorter events, 12.3 us)
Async XLA Ops:
  7.2 17.6 %copy-start.11 = (u32[32]{0:T(128)S(1)}, u32[32]{0:T(128)}, u32[]{:S(2)}) copy-start(u32[32]{0:T(128)} %constant.57) | copy-start | bytes 388
  7.2 45.3 %copy-start.4 = (bf16[256,128]{1,0:T(8,128)(2,1)S(1)}, bf16[256,128]{1,0:T(8,128)(2,1)}, u32[]{:S(2)}) copy-start(bf16[256,128]{1,0:T(8,128)(2,1)} %param.13) | copy-start | bytes 196612
  7.2 45.4 %copy-start = (bf16[256,1280]{1,0:T(8,128)(2,1)S(1)}, bf16[256,1280]{1,0:T(8,128)(2,1)}, u32[]{:S(2)}) copy-start(bf16[256,1280]{1,0:T(8,128)(2,1)} %param.10) | copy-start | bytes 1966084
  7.2 45.6 %copy-start.1 = (f32[1,20,64,128]{3,2,1,0:T(8,128)S(1)}, f32[1,20,64,128]{3,2,1,0:T(8,128)}, u32[]{:S(2)}) copy-start(f32[1,20,64,128]{3,2,1,0:T(8,128)} %param.16) | copy-start | bytes 1966084
  8.6 17.7 %copy-start.9 = (f32[20]{0:T(128)}, f32[20]{0:T(128)S(1)}, u32[]{:S(2)}) copy-start(f32[20]{0:T(128)S(1)} %neg.7) | copy-start | bytes 244
  12.1 5.4 %copy-start.7 = (f32[256,128]{0,1:T(8,128)}, f32[256,128]{0,1:T(8,128)S(1)}, u32[]{:S(2)}) copy-start(f32[256,128]{0,1:T(8,128)S(1)} %copy.54) | copy-start | bytes 393220
  12.1 41.7 %copy-start.5 = (bf16[256,128]{1,0:T(8,128)(2,1)S(1)}, bf16[256,128]{1,0:T(8,128)(2,1)}, u32[]{:S(2)}) copy-start(bf16[256,128]{1,0:T(8,128)(2,1)} %param.14) | copy-start | bytes 196612
  13.5 0.8 copy-start.2
  17.4 36.6 %all-to-all-start = ((f32[20,8,1024]{2,0,1:T(8,128)}), f32[20,8,1024]{2,0,1:T(8,128)S(1)}, u32[]{:S(2)}, u32[]{:S(2)}) async-start(f32[20,8,1024]{2,0,1:T(8,128)} %copy.56), calls=%async_computation | async-start | bytes 1572864 | tf_op jit(solution)/shard_map/all_to_all | solution.py:116
  53.8 25.7 %copy-start.8 = (pred[256,256]{1,0:T(8,128)(4,1)}, pred[256,256]{1,0:T(8,128)(4,1)S(1)}, u32[]{:S(2)}) copy-start(pred[256,256]{1,0:T(8,128)(4,1)S(1)} %fusion.36) | copy-start | bytes 196612
  67.6 19.0 %all-to-all-start.1 = ((f32[8,20,1,1024]{3,2,1,0:T(1,128)}), f32[8,20,1,1024]{3,2,1,0:T(1,128)S(1)}, u32[]{:S(2)}, u32[]{:S(2)}) async-start(f32[8,20,1,1024]{3,2,1,0:T(1,128)} %fusion.37), calls=%async_computation.1 | async-start | bytes 1310720 | tf_op jit(solution)/shard_map/all_to_all | solution.py:125
  72.1 54.2 %all-reduce.3.cloned.1.call-start = ((), (), s32[]{:S(2)}) async-start(), calls=%async_computation.2 | async-start | bytes 262144 | tf_op jit(solution)/shard_map/psum | solution.py:148
  75.6 3.9 %copy-start.3 = (bf16[256,1280]{0,1:T(8,128)(2,1)S(1)}, bf16[256,1280]{0,1:T(8,128)(2,1)}, u32[]{:S(2)}) copy-start(bf16[256,1280]{0,1:T(8,128)(2,1)} %copy-done.2) | copy-start | bytes 1966084
  75.6 3.9 %copy-start.6 = (f32[20,256]{1,0:T(8,128)S(1)}, f32[20,256]{1,0:T(8,128)}, u32[]{:S(2)}) copy-start(f32[20,256]{1,0:T(8,128)} %param.11) | copy-start | bytes 61444
  90.0 5.6 %copy-start.10 = (f32[20]{0:T(128)S(1)}, f32[20]{0:T(128)}, u32[]{:S(2)}) copy-start(f32[20]{0:T(128)} %get-tuple-element.159) | copy-start | bytes 244
Sparse Core Ops, SparseCore 0:
  95.2 31.1 all-reduce.2
